TPU v7x, 32 devices: a whole 2x2x4 slice. The times are simulated.
32 devices in a mesh: shell: 2 (over x), pix: 16 (over z, y, core).
Axes of the slice: x: 2, y: 2, z: 4, core: 2. Of those that a mesh axis runs over, the one named last changes fastest.
Arguments:
- block_tile: int32 [4, 1024], P('shell'), may hold values from 0 to 2047, as said below
- cell_index: int32 [4, 1024, 512], P('shell', 'pix'), may hold values from 0 to 2047
- masses: bfloat16 [4, 1024, 512], P('shell', 'pix'), may hold values from 0.125 to 8, as said below
- plane_coef: float32 [4], P('shell'), may hold values from 0.1 to 0.4
- plane_dist: float32 [4], P('shell'), may hold values from 0.2 to 1
- source_inv: float32 [4], P('shell'), may hold values from 0.5 to 1
Outputs:
- convergence: float32 [4, 2048, 2048], P('shell', 'pix')
- shear_one: float32 [4, 2048, 2048], P('shell', 'pix')
- shear_two: float32 [4, 2048, 2048], P('shell', 'pix')
Inputs may be any that keep to these rules, and one draw needn't show every extreme that they name: `block_tile`: each row is 16 aligned runs of 64 entries, one run per index of pix. The entries of a run are distinct, and at most 8 of them lie in one index's rows of tiles (tile b lies in the rows of index b // 128). In every plane some index receives exactly 8 tiles from every run. `masses`: positive particle weights.
All inputs are finite; a program needn't handle non-finite values.
Results may differ from a plain program's by a relative error of at most 0.0003.
Values sent between devices are 32-bit elements; how exact they have to be, the bound alone decides.
A program may use at most 64 MiB of HBM per device.

v0:
```python
from functools import partial
import math
import jax
import jax.numpy as jnp
from jax import lax
from jax.sharding import PartitionSpec as P

L = 2048
TR = 16
TC = 128
HIGHEST = lax.Precision.HIGHEST


def entering(value, axis, join, neutral):
    count, mine = (lax.axis_size(axis), lax.axis_index(axis))
    pieces = jax.tree.map(lambda part: lax.all_gather(part, axis), value)
    running = jax.tree.map(
        lambda part, zero: jnp.full_like(part, 0) + jnp.asarray(zero, part.dtype), value, neutral
    )

    def lap(position, running):
        longer = join(running, jax.tree.map(lambda part: part[position], pieces))
        return jax.tree.map(lambda new, old: jnp.where(position < mine, new, old), longer, running)

    return lax.fori_loop(0, count - 1, lap, running)


def dft_table(left_size, right_size, period, sign_value):
    left_idx = jnp.arange(left_size)[:, None]
    right_idx = jnp.arange(right_size)[None, :]
    angle = 2.0 * math.pi / period * (left_idx * right_idx % period).astype(jnp.float32)
    return (jnp.cos(angle), sign_value * jnp.sin(angle))


def mix_outer(table, real_part, imag_part):
    cosine, sine_part = table
    contract = partial(jnp.einsum, "ab,...bc->...ac", precision=HIGHEST)
    return (
        contract(cosine, real_part) - contract(sine_part, imag_part),
        contract(sine_part, real_part) + contract(cosine, imag_part),
    )


def mix_inner(table, real_part, imag_part):
    cosine, sine_part = table
    product = partial(jnp.matmul, precision=HIGHEST)
    return (
        product(real_part, cosine) - product(imag_part, sine_part),
        product(real_part, sine_part) + product(imag_part, cosine),
    )


def twist(table, real_part, imag_part):
    cosine, sine_part = table
    return (real_part * cosine - imag_part * sine_part, real_part * sine_part + imag_part * cosine)


def transform_last(real_part, imag_part, sign_value):
    length = real_part.shape[-1]
    inner = math.gcd(length, 128)
    outer = length // inner
    leading = real_part.shape[:-1]
    real_part = real_part.reshape(leading + (outer, inner))
    imag_part = imag_part.reshape(leading + (outer, inner))
    outer_table = dft_table(outer, outer, outer, sign_value)
    inner_table = dft_table(inner, inner, inner, sign_value)
    twiddle = dft_table(outer, inner, length, sign_value)
    if sign_value < 0:
        real_part, imag_part = mix_outer(outer_table, real_part, imag_part)
        real_part, imag_part = twist(twiddle, real_part, imag_part)
        real_part, imag_part = mix_inner(inner_table, real_part, imag_part)
    else:
        real_part, imag_part = mix_inner(inner_table, real_part, imag_part)
        real_part, imag_part = twist(twiddle, real_part, imag_part)
        real_part, imag_part = mix_outer(outer_table, real_part, imag_part)
    return (real_part.reshape(leading + (length,)), imag_part.reshape(leading + (length,)))


def frequency_of(position, length):
    inner = math.gcd(length, 128)
    outer = length // inner
    frequency = position // inner + outer * (position % inner)
    signed = jnp.where(frequency >= length // 2, frequency - length, frequency).astype(jnp.float32)
    keep_mask = (frequency != length // 2).astype(jnp.float32)
    return (signed, keep_mask)


def add_pairs(earlier_pair, later_pair):
    return (earlier_pair[0] + later_pair[0], earlier_pair[1] + later_pair[1])


def deposit_group(item):
    cell_ids, weights = item
    tile_rows = cell_ids // TC
    tile_cols = cell_ids % TC
    row_hot = jnp.where(
        tile_rows[:, None, :] == jnp.arange(TR)[None, :, None],
        weights[:, None, :],
        jnp.zeros((), jnp.bfloat16),
    )
    col_hot = (tile_cols[:, :, None] == jnp.arange(TC)[None, None, :]).astype(jnp.bfloat16)
    return jnp.einsum("grk,gkc->grc", row_hot, col_hot, preferred_element_type=jnp.float32)


def rows_to_sending(packed, groups, slab, cols_own):
    count, fields = (packed.shape[0], packed.shape[1])
    return (
        packed.reshape(count, fields, slab, groups, cols_own)
        .transpose(3, 0, 1, 4, 2)
        .reshape(groups, count, fields, cols_own * slab)
    )


def arrived_to_columns(arrived, groups, slab, cols_own):
    count, fields = (arrived.shape[1], arrived.shape[2])
    return (
        arrived.reshape(groups, count, fields, cols_own, slab)
        .transpose(1, 2, 3, 0, 4)
        .reshape(count, fields, cols_own, groups * slab)
    )


def columns_to_sending(stacked, groups, slab, cols_own):
    count, fields = (stacked.shape[0], stacked.shape[1])
    return (
        stacked.reshape(count, fields, cols_own, groups, slab)
        .transpose(3, 0, 1, 2, 4)
        .reshape(groups, count, fields, cols_own * slab)
    )


def landed_to_rows(landed, groups, slab, cols_own):
    count, fields = (landed.shape[1], landed.shape[2])
    return (
        landed.reshape(groups, count, fields, cols_own, slab)
        .transpose(1, 2, 4, 0, 3)
        .reshape(count, fields, slab, groups * cols_own)
    )


def local(block_tile, cell_index, masses, plane_coef, plane_dist, source_inv):
    groups = lax.axis_size("pix")
    my_index = lax.axis_index("pix")
    planes, local_tiles, per_tile = cell_index.shape
    slab = L // groups
    per_owner = slab // TR * (L // TC)
    cap = max(1, 2 * local_tiles // groups)
    flat = TR * TC
    batch_tiles = 8
    deposited = lax.map(
        deposit_group,
        (cell_index.reshape(-1, batch_tiles, per_tile), masses.reshape(-1, batch_tiles, per_tile)),
    )
    tile_sums = deposited.reshape(planes, local_tiles, flat)
    table = block_tile.reshape(planes, groups, local_tiles)
    owner = table // per_owner
    earlier = jnp.arange(local_tiles)[:, None] < jnp.arange(local_tiles)[None, :]
    same_owner = owner[:, :, :, None] == owner[:, :, None, :]
    rank = jnp.sum(jnp.where(same_owner & earlier[None, None], 1, 0), axis=2)
    slot = owner * cap + rank
    my_slots = lax.dynamic_index_in_dim(slot, my_index, axis=1, keepdims=False)
    slot_grid = jnp.arange(groups)[:, None] * cap + jnp.arange(cap)[None, :]
    send_hot = (my_slots[:, None, None, :] == slot_grid[None, :, :, None]).astype(jnp.float32)
    outgoing = jnp.einsum("pnct,ptf->npcf", send_hot, tile_sums, precision=HIGHEST)
    incoming = lax.all_to_all(outgoing, "pix", split_axis=0, concat_axis=0, tiled=True)
    local_index = table - my_index * per_owner
    is_mine = owner == my_index
    tile_hot = (is_mine[..., None] & (local_index[..., None] == jnp.arange(per_owner))).astype(
        jnp.float32
    )
    slot_hot = (rank[..., None] == jnp.arange(cap)).astype(jnp.float32)
    placing = jnp.einsum("pstl,pstc->plsc", tile_hot, slot_hot, precision=HIGHEST)
    slab_tiles = jnp.einsum("plsc,spcf->plf", placing, incoming, precision=HIGHEST)
    density = (
        slab_tiles.reshape(planes, slab // TR, L // TC, TR, TC)
        .transpose(0, 1, 3, 2, 4)
        .reshape(planes, slab, L)
    )
    total = lax.psum(jnp.sum(density, axis=(1, 2)), "pix")
    contrast = density / (total / (L * L))[:, None, None] - 1.0
    near_local = jnp.cumsum(plane_coef[:, None, None] * contrast, axis=0)
    far_local = jnp.cumsum((plane_coef * plane_dist)[:, None, None] * contrast, axis=0)
    blank = jnp.zeros((slab, L), jnp.float32)
    near_before, far_before = entering(
        (near_local[-1], far_local[-1]), "shell", add_pairs, (blank, blank)
    )
    convergence = near_before + near_local - source_inv[:, None, None] * (far_before + far_local)
    cols_own = L // groups
    wave_x, keep_x = frequency_of(my_index * cols_own + jnp.arange(cols_own), L)
    wave_y, keep_y = frequency_of(jnp.arange(L), L)
    wave_x = wave_x[:, None]
    wave_y = wave_y[None, :]
    both_keep = keep_x[:, None] * keep_y[None, :]
    wave_power = jnp.maximum(wave_x * wave_x + wave_y * wave_y, 1.0)
    kernel_one = both_keep * (wave_x * wave_x - wave_y * wave_y) / wave_power
    kernel_two = both_keep * 2.0 * wave_x * wave_y / wave_power
    scale = 1.0 / (L * L)
    spec_real, spec_imag = transform_last(convergence[0::2], convergence[1::2], -1.0)
    sending = rows_to_sending(jnp.stack([spec_real, spec_imag], axis=1), groups, slab, cols_own)
    arrived = lax.all_to_all(sending, "pix", split_axis=0, concat_axis=0, tiled=True)
    columns = arrived_to_columns(arrived, groups, slab, cols_own)
    row_real, row_imag = transform_last(columns[:, 0], columns[:, 1], -1.0)
    first_real, first_imag = transform_last(row_real * kernel_one, row_imag * kernel_one, 1.0)
    second_real, second_imag = transform_last(row_real * kernel_two, row_imag * kernel_two, 1.0)
    stacked = jnp.stack([first_real, first_imag, second_real, second_imag], axis=1)
    landed = lax.all_to_all(
        columns_to_sending(stacked, groups, slab, cols_own),
        "pix",
        split_axis=0,
        concat_axis=0,
        tiled=True,
    )
    row_layout = landed_to_rows(landed, groups, slab, cols_own)
    even_one, odd_one = transform_last(row_layout[:, 0], row_layout[:, 1], 1.0)
    even_two, odd_two = transform_last(row_layout[:, 2], row_layout[:, 3], 1.0)
    shear_one = jnp.stack([even_one, odd_one], axis=1).reshape(planes, slab, L)
    shear_two = jnp.stack([even_two, odd_two], axis=1).reshape(planes, slab, L)
    return (convergence, shear_one * scale, shear_two * scale)


def solution(mesh):
    placed = (
        P("shell", None),
        P("shell", "pix", None),
        P("shell", "pix", None),
        P("shell"),
        P("shell"),
        P("shell"),
    )
    return jax.shard_map(
        local,
        mesh=mesh,
        in_specs=placed,
        out_specs=(P("shell", "pix", None), P("shell", "pix", None), P("shell", "pix", None)),
        check_vma=False,
    )
```

profile of v0, /device:TPU:1, one launch (start us, length us, event | category | flops | bytes accessed | tf_op | source)
XLA Modules:
  0.0 498.4 jit_solution(13083244063688740668)
XLA Ops:
  8.0 56.0 %while.8 = (s32[]{:T(128)}, f32[16,8,16,128]{3,2,1,0:T(8,128)S(1)}, s32[16,8,512]{2,1,0:T(8,128)}, bf16[16,8,512]{2,1,0:T(8,128)(2,1)}, s32[]{:T(128)}) while((s32[]{:T(128)}, f32[16,8,16,128]{3,2,1,0:T(8,128)S(1)}, s32[16,8,512]{2,1,0:T(8,128)}, bf16[16,8,512]{2,1,0:T(8,128)(2,1)}, s32[]{:T(128)}) %tuple.63), condition=%wide.region_2.3_spmd, body=%wide.region_1.2_spmd.sunk | while | flops 17534976 | bytes 196693 | solution.py:150
  65.7 2.5 copy.183
  68.2 7.3 %all-to-all-start = ((f32[16,2,8,2048]{3,2,1,0:T(8,128)}), f32[16,2,8,2048]{3,2,1,0:T(8,128)S(1)}, u32[]{:S(2)}, u32[]{:S(2)}) async-start(f32[16,2,8,2048]{3,2,1,0:T(8,128)} %copy.183), calls=%async_computation | async-start | bytes 4194304 | tf_op jit(solution)/shard_map/all_to_all | solution.py:165
  76.9 40.2 %all-to-all-done = f32[16,2,8,2048]{3,2,1,0:T(8,128)S(1)} async-done(((f32[16,2,8,2048]{3,2,1,0:T(8,128)}), f32[16,2,8,2048]{3,2,1,0:T(8,128)S(1)}, u32[]{:S(2)}, u32[]{:S(2)}) %all-to-all-start) | async-done | bytes 2097184 | tf_op jit(solution)/shard_map/all_to_all | solution.py:165
  117.1 3.2 bitcast_reduce_fusion
  120.3 33.9 %psum.7 = f32[2]{0:T(128)S(1)} all-reduce(f32[2]{0:T(128)S(1)} %get-tuple-element.117), channel_id=1, replica_groups=mesh['shell'=2,'pix'=16] {'pix'}, use_global_device_ids=true, to_apply=%region_4.5 | all-reduce | flops 2 | bytes 16 | tf_op jit(solution)/shard_map/psum | solution.py:179
  154.2 2.0 copy.236
  156.2 2.0 copy.185
  165.7 31.5 %all-gather.3.cloned.1.call-done = f32[2,128,2048]{2,1,0:T(8,128)} async-done(((f32[1,128,2048]{2,1,0:T(8,128)}), f32[2,128,2048]{2,1,0:T(8,128)}) %all-gather.3.cloned.1.call-update) | async-done | bytes 2097168 | tf_op jit(solution)/shard_map/all_gather | solution.py:16
  198.6 33.9 %all-gather.5.cloned.1.call-done = f32[2,128,2048]{2,1,0:T(8,128)} async-done(((f32[1,128,2048]{2,1,0:T(8,128)}), f32[2,128,2048]{2,1,0:T(8,128)}) %all-gather.5.cloned.1.call-update) | async-done | bytes 2097168 | tf_op jit(solution)/shard_map/all_gather | solution.py:16
  245.7 2.0 fusion.31
  249.7 6.4 %all-to-all-start.1 = ((f32[16,1,2,16384]{3,1,2,0:T(1,128)}), f32[16,1,2,16384]{3,1,2,0:T(1,128)S(1)}, u32[]{:S(2)}, u32[]{:S(2)}) async-start(f32[16,1,2,16384]{3,1,2,0:T(1,128)} %bitcast.319), calls=%async_computation.1 | async-start | bytes 4194304 | tf_op jit(solution)/shard_map/all_to_all | solution.py:200
  256.2 41.4 %all-to-all-done.1 = f32[16,1,2,16384]{3,1,2,0:T(1,128)S(1)} async-done(((f32[16,1,2,16384]{3,1,2,0:T(1,128)}), f32[16,1,2,16384]{3,1,2,0:T(1,128)S(1)}, u32[]{:S(2)}, u32[]{:S(2)}) %all-to-all-start.1) | async-done | bytes 2097184 | tf_op jit(solution)/shard_map/all_to_all | solution.py:200
  299.4 2.6 fusion.465
  324.5 1.9 multiply_add_fusion.3
  326.4 2.0 fusion.65
  341.7 103.1 %all_to_all.15 = f32[16,1,4,16384]{3,1,2,0:T(1,128)S(1)} all-to-all(f32[16,1,4,16384]{3,1,2,0:T(1,128)S(1)} %bitcast.304), channel_id=1, replica_groups=mesh['shell'=2,'pix'=16] {'pix'}, dimensions={0} | all-to-all | bytes 8388608 | tf_op jit(solution)/shard_map/all_to_all | solution.py:206
  445.6 1.9 fusion.91
  447.6 1.9 fusion.108
  449.5 1.9 fusion.94
  451.4 1.9 fusion.111
  453.4 2.0 convolution_subtract_fusion.3
  455.4 2.2 convolution_add_fusion.3
  457.5 2.0 convolution_subtract_fusion.1
  459.5 2.3 multiply_add_fusion
  468.3 2.8 fusion.22
  471.2 2.6 fusion.21
  473.8 2.4 stack_reshape.21
  476.2 2.4 stack_reshape.20
  478.5 2.6 fusion.24
  481.1 2.6 fusion.23
  483.7 2.5 stack_reshape.9
  (170 shorter events, 133.2 us)
Async XLA Ops:
  68.2 48.9 %all-to-all-start = ((f32[16,2,8,2048]{3,2,1,0:T(8,128)}), f32[16,2,8,2048]{3,2,1,0:T(8,128)S(1)}, u32[]{:S(2)}, u32[]{:S(2)}) async-start(f32[16,2,8,2048]{3,2,1,0:T(8,128)} %copy.183), calls=%async_computation | async-start | bytes 4194304 | tf_op jit(solution)/shard_map/all_to_all | solution.py:165
  75.6 121.7 %all-gather.3.cloned.1.call-start = ((), (), s32[]{:S(2)}) async-start(), calls=%async_computation.3 | async-start | bytes 3145728 | tf_op jit(solution)/shard_map/all_gather | solution.py:16
  158.2 1.7 copy-start.10
  160.2 1.3 copy-start
  161.6 1.4 copy-start.12
  162.7 69.9 %all-gather.5.cloned.1.call-start = ((), (), s32[]{:S(2)}) async-start(), calls=%async_computation.4 | async-start | bytes 3145728 | tf_op jit(solution)/shard_map/all_gather | solution.py:16
  163.3 1.3 copy-start.2
  165.7 68.3 %copy-start.1 = (f32[2,128,2048]{2,1,0:T(8,128)S(1)}, f32[2,128,2048]{2,1,0:T(8,128)}, u32[]{:S(2)}) copy-start(f32[2,128,2048]{2,1,0:T(8,128)} %copy-done) | copy-start | bytes 6291460
  165.7 68.3 %copy-start.11 = (f32[2]{0:T(128)S(1)}, f32[2]{0:T(128)}, u32[]{:S(2)}) copy-start(f32[2]{0:T(128)} %param.13) | copy-start | bytes 28
  232.5 1.9 copy-start.3
  235.1 1.3 copy-start.4
  249.7 47.9 %all-to-all-start.1 = ((f32[16,1,2,16384]{3,1,2,0:T(1,128)}), f32[16,1,2,16384]{3,1,2,0:T(1,128)S(1)}, u32[]{:S(2)}, u32[]{:S(2)}) async-start(f32[16,1,2,16384]{3,1,2,0:T(1,128)} %bitcast.319), calls=%async_computation.1 | async-start | bytes 4194304 | tf_op jit(solution)/shard_map/all_to_all | solution.py:200
  481.1 5.1 %copy-start.5 = (f32[1,128,16,128]{3,2,1,0:T(8,128)S(1)}, f32[1,128,16,128]{3,2,1,0:T(8,128)}, u32[]{:S(2)}) copy-start(f32[1,128,16,128]{3,2,1,0:T(8,128)} %fusion.24) | copy-start | bytes 3145732
  483.7 3.7 copy-start.6
  483.7 3.7 copy-start.7
  487.4 1.5 copy-start.8
  487.4 2.3 copy-start.9
Sparse Core Ops, SparseCore 0:
  162.8 34.4 all-gather.2
  199.4 33.0 all-gather.4
where the time goes:
time: 508 us; the launch traced here: 498 us
  waiting for transfers between devices  147 us (29%)
  blocking collectives  137 us (27%)
  matrix products  106 us (21%)
  local copies, waits for them, and re-layouts  47.2 us (9%)
  other arithmetic  31.7 us (6%)
  between operations  15.1 us (3%)
  starting transfers between devices  14 us (3%)
    all_to_all x1, blocking collectives, local(): lax.all_to_all(columns_to_sending(stacked, groups, slab, cols_own), 'pix'...  103 us
    all_gather x2, waiting for transfers between devices, entering(): pieces = jax.tree.map(lambda part: lax.all_gather(part, axis), value)  65.5 us
    all_to_all x1, waiting for transfers between devices, local(): lax.all_to_all(sending, 'pix', split_axis=0, concat_axis=0, tiled=True)  41.4 us
    all_to_all x1, waiting for transfers between devices, local(): lax.all_to_all(outgoing, 'pix', split_axis=0, concat_axis=0, tiled=True)  40.2 us
    psum x1, blocking collectives, local(): total = lax.psum(jnp.sum(density, axis=(1, 2)), 'pix')  33.9 us
    dot_general x16, matrix products, deposit_group(): jnp.einsum('grk,gkc->grc', row_hot, col_hot, preferred_element_type=jnp.f...  21.1 us
    select_n x16, other arithmetic, deposit_group(): tile_cols = cell_ids % TC  11.7 us
    select_n x16, other arithmetic, deposit_group(): tile_rows = cell_ids // TC  11.7 us
  transfers between devices with their start and end apart: 4, of which 4 were waited for; matrix products, arithmetic and copies ran while one was open for 1% of the time, Pallas kernels for 0%

commit v1 on v0

--- a/solution.py
+++ b/solution.py
@@ -9,6 +9,22 @@
 TR = 16
 TC = 128
 HIGHEST = lax.Precision.HIGHEST
+
+
+def pairwise_exchange(shard, axis, split, join):
+    ways, here = (lax.axis_size(axis), lax.axis_index(axis))
+    width = shard.shape[split] // ways
+    shape = list(shard.shape)
+    shape[split] = width
+    height = shape[join]
+    shape[join] = height * ways
+    full = jnp.zeros(shape, shard.dtype)
+    for mask in range(ways):
+        part = lax.dynamic_slice_in_dim(shard, (here ^ mask) * width, width, axis=split)
+        if mask:
+            part = lax.ppermute(part, axis, [(d, d ^ mask) for d in range(ways)])
+        full = lax.dynamic_update_slice_in_dim(full, part, (here ^ mask) * height, axis=join)
+    return full
 
 
 def entering(value, axis, join, neutral):
@@ -197,7 +213,7 @@
     scale = 1.0 / (L * L)
     spec_real, spec_imag = transform_last(convergence[0::2], convergence[1::2], -1.0)
     sending = rows_to_sending(jnp.stack([spec_real, spec_imag], axis=1), groups, slab, cols_own)
-    arrived = lax.all_to_all(sending, "pix", split_axis=0, concat_axis=0, tiled=True)
+    arrived = pairwise_exchange(sending, "pix", 0, 0)
     columns = arrived_to_columns(arrived, groups, slab, cols_own)
     row_real, row_imag = transform_last(columns[:, 0], columns[:, 1], -1.0)
     first_real, first_imag = transform_last(row_real * kernel_one, row_imag * kernel_one, 1.0)

time: 508 us -> 541 us (1.065)
  local copies, waits for them, and re-layouts: 47.2 us -> 61.6 us
  starting transfers between devices: 14 us -> 27.8 us
  waiting for transfers between devices: 147 us -> 156 us
  blocking collectives: 137 us -> 131 us
    ppermute x0 -> x15, waiting for transfers between devices: none -> 50.4 us  [pairwise_exchange(): part = lax.ppermute(part, axis, [(d, d ^ mask) for d in range(ways)])]
    all_to_all x1 -> x0, waiting for transfers between devices: 41.4 us -> none  [local(): lax.all_to_all(sending, 'pix', split_axis=0, concat_axis=0, tiled=True)]
    ppermute x0 -> x15, starting transfers between devices: none -> 20.2 us  [pairwise_exchange(): part = lax.ppermute(part, axis, [(d, d ^ mask) for d in range(ways)])]
    dynamic_update_slice x0 -> x15, local copies, waits for them, and re-layouts: none -> 9.96 us  [pairwise_exchange(): lax.dynamic_update_slice_in_dim(full, part, (here ^ mask) * height, axis=...]
    all_to_all x1 -> x0, starting transfers between devices: 6.38 us -> none  [local(): lax.all_to_all(sending, 'pix', split_axis=0, concat_axis=0, tiled=True)]
    all_to_all x1, blocking collectives: 103 us -> 97.6 us  [local(): lax.all_to_all(columns_to_sending(stacked, groups, slab, cols_own), 'pix'...]
  transfers between devices with their start and end apart: 4 -> 18, of which waited for: 4 -> 13; matrix products, arithmetic and copies ran while one was open for 1% -> 3% of each run, Pallas kernels for 0% -> 0%
where the time goes in v1:
time: 541 us; the launch traced here: 531 us
  waiting for transfers between devices  156 us (29%)
  blocking collectives  131 us (24%)
  matrix products  106 us (20%)
  local copies, waits for them, and re-layouts  61.6 us (11%)
  other arithmetic  33 us (6%)
  starting transfers between devices  27.8 us (5%)
  between operations  15.3 us (3%)
    all_to_all x1, blocking collectives, local(): lax.all_to_all(columns_to_sending(stacked, groups, slab, cols_own), 'pix'...  97.6 us
    all_gather x2, waiting for transfers between devices, entering(): pieces = jax.tree.map(lambda part: lax.all_gather(part, axis), value)  65.3 us
    ppermute x15, waiting for transfers between devices, pairwise_exchange(): part = lax.ppermute(part, axis, [(d, d ^ mask) for d in range(ways)])  50.4 us
    all_to_all x1, waiting for transfers between devices, local(): lax.all_to_all(outgoing, 'pix', split_axis=0, concat_axis=0, tiled=True)  40.2 us
    psum x1, blocking collectives, local(): total = lax.psum(jnp.sum(density, axis=(1, 2)), 'pix')  33.9 us
    dot_general x16, matrix products, deposit_group(): jnp.einsum('grk,gkc->grc', row_hot, col_hot, preferred_element_type=jnp.f...  21.1 us
    ppermute x15, starting transfers between devices, pairwise_exchange(): part = lax.ppermute(part, axis, [(d, d ^ mask) for d in range(ways)])  20.2 us
    select_n x16, other arithmetic, deposit_group(): tile_cols = cell_ids % TC  11.7 us
  transfers between devices with their start and end apart: 18, of which 13 were waited for; matrix products, arithmetic and copies ran while one was open for 3% of the time, Pallas kernels for 0%

profile of v1, /device:TPU:1, one launch (start us, length us, event | category | flops | bytes accessed | tf_op | source)
XLA Modules:
  0.0 531.2 jit_solution(5946017822149868616)
XLA Ops:
  8.0 56.0 %while.8 = (s32[]{:T(128)}, f32[16,8,16,128]{3,2,1,0:T(8,128)S(1)}, s32[16,8,512]{2,1,0:T(8,128)}, bf16[16,8,512]{2,1,0:T(8,128)(2,1)}, s32[]{:T(128)}) while((s32[]{:T(128)}, f32[16,8,16,128]{3,2,1,0:T(8,128)S(1)}, s32[16,8,512]{2,1,0:T(8,128)}, bf16[16,8,512]{2,1,0:T(8,128)(2,1)}, s32[]{:T(128)}) %tuple.78), condition=%wide.region_2.3_spmd, body=%wide.region_1.2_spmd.sunk | while | flops 17534976 | bytes 196693 | solution.py:166
  65.7 2.5 copy.183
  68.2 7.3 %all-to-all-start = ((f32[16,2,8,2048]{3,2,1,0:T(8,128)}), f32[16,2,8,2048]{3,2,1,0:T(8,128)S(1)}, u32[]{:S(2)}, u32[]{:S(2)}) async-start(f32[16,2,8,2048]{3,2,1,0:T(8,128)} %copy.183), calls=%async_computation | async-start | bytes 4194304 | tf_op jit(solution)/shard_map/all_to_all | solution.py:181
  76.9 40.2 %all-to-all-done = f32[16,2,8,2048]{3,2,1,0:T(8,128)S(1)} async-done(((f32[16,2,8,2048]{3,2,1,0:T(8,128)}), f32[16,2,8,2048]{3,2,1,0:T(8,128)S(1)}, u32[]{:S(2)}, u32[]{:S(2)}) %all-to-all-start) | async-done | bytes 2097184 | tf_op jit(solution)/shard_map/all_to_all | solution.py:181
  117.1 3.2 bitcast_reduce_fusion
  120.3 33.9 %psum.7 = f32[2]{0:T(128)S(1)} all-reduce(f32[2]{0:T(128)S(1)} %get-tuple-element.133), channel_id=1, replica_groups=mesh['shell'=2,'pix'=16] {'pix'}, use_global_device_ids=true, to_apply=%region_4.5 | all-reduce | flops 2 | bytes 16 | tf_op jit(solution)/shard_map/psum | solution.py:195
  166.0 31.4 %all-gather.3.cloned.1.call-done = f32[2,128,2048]{2,1,0:T(8,128)} async-done(((f32[1,128,2048]{2,1,0:T(8,128)}), f32[2,128,2048]{2,1,0:T(8,128)}) %all-gather.3.cloned.1.call-update) | async-done | bytes 2097168 | tf_op jit(solution)/shard_map/all_gather | solution.py:32
  198.6 33.9 %all-gather.5.cloned.1.call-done = f32[2,128,2048]{2,1,0:T(8,128)} async-done(((f32[1,128,2048]{2,1,0:T(8,128)}), f32[2,128,2048]{2,1,0:T(8,128)}) %all-gather.5.cloned.1.call-update) | async-done | bytes 2097168 | tf_op jit(solution)/shard_map/all_gather | solution.py:32
  251.0 3.3 broadcast_in_dim.53
  254.3 2.5 constant_dynamic-slice_fusion
  257.6 3.9 collective-permute-start.14
  261.8 3.7 collective-permute-start.12
  267.5 5.1 collective-permute-done.1
  274.0 4.2 collective-permute-done.2
  278.9 4.0 collective-permute-done.3
  284.7 3.7 collective-permute-done.4
  290.2 2.9 collective-permute-done.5
  293.2 3.1 collective-permute-start.6
  296.9 2.7 collective-permute-done.6
  299.7 2.8 collective-permute-start.7
  303.1 5.2 collective-permute-done.7
  309.9 7.5 %collective-permute-done.8 = f32[1,1,2,16384]{3,1,2,0:T(1,128)S(1)} collective-permute-done((f32[1,1,2,16384]{3,1,2,0:T(1,128)S(1)}, f32[1,1,2,16384]{3,1,2,0:T(1,128)S(1)}, u32[]{:S(2)}, u32[]{:S(2)}) %collective-permute-start.8) | collective-permute-done | bytes 131104 | tf_op jit(solution)/shard_map/ppermute | solution.py:25
  318.3 8.0 %collective-permute-done.9 = f32[1,1,2,16384]{3,1,2,0:T(1,128)S(1)} collective-permute-done((f32[1,1,2,16384]{3,1,2,0:T(1,128)S(1)}, f32[1,1,2,16384]{3,1,2,0:T(1,128)S(1)}, u32[]{:S(2)}, u32[]{:S(2)}) %collective-permute-start.9) | collective-permute-done | bytes 131104 | tf_op jit(solution)/shard_map/ppermute | solution.py:25
  327.0 7.0 %collective-permute-done.10 = f32[1,1,2,16384]{3,1,2,0:T(1,128)S(1)} collective-permute-done((f32[1,1,2,16384]{3,1,2,0:T(1,128)S(1)}, f32[1,1,2,16384]{3,1,2,0:T(1,128)S(1)}, u32[]{:S(2)}, u32[]{:S(2)}) %collective-permute-start.10) | collective-permute-done | bytes 131104 | tf_op jit(solution)/shard_map/ppermute | solution.py:25
  380.1 97.6 %all_to_all.10 = f32[16,1,4,16384]{3,1,2,0:T(1,128)S(1)} all-to-all(f32[16,1,4,16384]{3,1,2,0:T(1,128)S(1)} %bitcast.304), channel_id=1, replica_groups=mesh['shell'=2,'pix'=16] {'pix'}, dimensions={0} | all-to-all | bytes 8388608 | tf_op jit(solution)/shard_map/all_to_all | solution.py:222
  501.2 2.8 fusion.22
  504.0 2.6 fusion.21
  506.6 2.4 stack_reshape.21
  509.0 2.3 stack_reshape.20
  511.3 2.6 fusion.24
  513.9 2.6 fusion.23
  516.5 2.5 stack_reshape.9
  (215 shorter events, 178.3 us)
Async XLA Ops:
  68.2 48.9 %all-to-all-start = ((f32[16,2,8,2048]{3,2,1,0:T(8,128)}), f32[16,2,8,2048]{3,2,1,0:T(8,128)S(1)}, u32[]{:S(2)}, u32[]{:S(2)}) async-start(f32[16,2,8,2048]{3,2,1,0:T(8,128)} %copy.183), calls=%async_computation | async-start | bytes 4194304 | tf_op jit(solution)/shard_map/all_to_all | solution.py:181
  75.6 121.7 %all-gather.3.cloned.1.call-start = ((), (), s32[]{:S(2)}) async-start(), calls=%async_computation.2 | async-start | bytes 3145728 | tf_op jit(solution)/shard_map/all_gather | solution.py:32
  158.2 1.7 copy-start.10
  160.2 1.3 copy-start
  161.6 1.4 copy-start.12
  162.7 69.9 %all-gather.5.cloned.1.call-start = ((), (), s32[]{:S(2)}) async-start(), calls=%async_computation.3 | async-start | bytes 3145728 | tf_op jit(solution)/shard_map/all_gather | solution.py:32
  163.3 1.3 copy-start.2
  165.9 68.1 %copy-start.1 = (f32[2,128,2048]{2,1,0:T(8,128)S(1)}, f32[2,128,2048]{2,1,0:T(8,128)}, u32[]{:S(2)}) copy-start(f32[2,128,2048]{2,1,0:T(8,128)} %copy-done) | copy-start | bytes 6291460
  165.9 68.1 %copy-start.11 = (f32[2]{0:T(128)S(1)}, f32[2]{0:T(128)}, u32[]{:S(2)}) copy-start(f32[2]{0:T(128)} %param.13) | copy-start | bytes 28
  232.6 1.9 copy-start.3
  235.2 1.3 copy-start.4
  256.8 8.9 %collective-permute-start = (f32[1,1,2,16384]{3,1,2,0:T(1,128)S(1)}, f32[1,1,2,16384]{3,1,2,0:T(1,128)S(1)}, u32[]{:S(2)}, u32[]{:S(2)}) collective-permute-start(f32[1,1,2,16384]{3,1,2,0:T(1,128)S(1)} %get-tuple-element.125), channel_id=1, source_target_pairs={{0,1},{1,0},{2,3},{3,2},{4,5},{5,4},{6,7},{7,6},{8,9},{9,8},{10,11... | collective-permute-start | bytes 393224 | tf_op jit(solution)/shard_map/ppermute | solution.py:25
  257.6 79.0 %collective-permute-start.14 = (f32[1,1,2,16384]{3,1,2,0:T(1,128)S(1)}, f32[1,1,2,16384]{3,1,2,0:T(1,128)S(1)}, u32[]{:S(2)}, u32[]{:S(2)}) collective-permute-start(f32[1,1,2,16384]{3,1,2,0:T(1,128)S(1)} %get-tuple-element.111), channel_id=1, source_target_pairs={{0,15},{1,14},{2,13},{3,12},{4,11},{5,10},{6,9},{7,8},{8,7},{9,6},... | collective-permute-start | bytes 393224 | tf_op jit(solution)/shard_map/ppermute | solution.py:25
  261.6 74.4 %collective-permute-start.13 = (f32[1,1,2,16384]{3,1,2,0:T(1,128)S(1)}, f32[1,1,2,16384]{3,1,2,0:T(1,128)S(1)}, u32[]{:S(2)}, u32[]{:S(2)}) collective-permute-start(f32[1,1,2,16384]{3,1,2,0:T(1,128)S(1)} %get-tuple-element.112), channel_id=1, source_target_pairs={{0,14},{1,15},{2,12},{3,13},{4,10},{5,11},{6,8},{7,9},{8,6},{9,7},... | collective-permute-start | bytes 393224 | tf_op jit(solution)/shard_map/ppermute | solution.py:25
  261.8 73.6 %collective-permute-start.12 = (f32[1,1,2,16384]{3,1,2,0:T(1,128)S(1)}, f32[1,1,2,16384]{3,1,2,0:T(1,128)S(1)}, u32[]{:S(2)}, u32[]{:S(2)}) collective-permute-start(f32[1,1,2,16384]{3,1,2,0:T(1,128)S(1)} %get-tuple-element.113), channel_id=1, source_target_pairs={{0,13},{1,12},{2,15},{3,14},{4,9},{5,8},{6,11},{7,10},{8,5},{9,4},... | collective-permute-start | bytes 393224 | tf_op jit(solution)/shard_map/ppermute | solution.py:25
  265.5 69.2 %collective-permute-start.11 = (f32[1,1,2,16384]{3,1,2,0:T(1,128)S(1)}, f32[1,1,2,16384]{3,1,2,0:T(1,128)S(1)}, u32[]{:S(2)}, u32[]{:S(2)}) collective-permute-start(f32[1,1,2,16384]{3,1,2,0:T(1,128)S(1)} %get-tuple-element.114), channel_id=1, source_target_pairs={{0,12},{1,13},{2,14},{3,15},{4,8},{5,9},{6,10},{7,11},{8,4},{9,5},... | collective-permute-start | bytes 393224 | tf_op jit(solution)/shard_map/ppermute | solution.py:25
  265.7 6.9 %collective-permute-start.1 = (f32[1,1,2,16384]{3,1,2,0:T(1,128)S(1)}, f32[1,1,2,16384]{3,1,2,0:T(1,128)S(1)}, u32[]{:S(2)}, u32[]{:S(2)}) collective-permute-start(f32[1,1,2,16384]{3,1,2,0:T(1,128)S(1)} %get-tuple-element.124), channel_id=1, source_target_pairs={{0,2},{1,3},{2,0},{3,1},{4,6},{5,7},{6,4},{7,5},{8,10},{9,11},{10,... | collective-permute-start | bytes 393224 | tf_op jit(solution)/shard_map/ppermute | solution.py:25
  272.6 5.6 %collective-permute-start.2 = (f32[1,1,2,16384]{3,1,2,0:T(1,128)S(1)}, f32[1,1,2,16384]{3,1,2,0:T(1,128)S(1)}, u32[]{:S(2)}, u32[]{:S(2)}) collective-permute-start(f32[1,1,2,16384]{3,1,2,0:T(1,128)S(1)} %get-tuple-element.123), channel_id=1, source_target_pairs={{0,3},{1,2},{2,1},{3,0},{4,7},{5,6},{6,5},{7,4},{8,11},{9,10},{10,... | collective-permute-start | bytes 393224 | tf_op jit(solution)/shard_map/ppermute | solution.py:25
  278.2 4.7 collective-permute-start.3
  282.9 5.5 %collective-permute-start.4 = (f32[1,1,2,16384]{3,1,2,0:T(1,128)S(1)}, f32[1,1,2,16384]{3,1,2,0:T(1,128)S(1)}, u32[]{:S(2)}, u32[]{:S(2)}) collective-permute-start(f32[1,1,2,16384]{3,1,2,0:T(1,128)S(1)} %get-tuple-element.121), channel_id=1, source_target_pairs={{0,5},{1,4},{2,7},{3,6},{4,1},{5,0},{6,3},{7,2},{8,13},{9,12},{10,... | collective-permute-start | bytes 393224 | tf_op jit(solution)/shard_map/ppermute | solution.py:25
  288.4 4.7 collective-permute-start.5
  293.2 6.5 %collective-permute-start.6 = (f32[1,1,2,16384]{3,1,2,0:T(1,128)S(1)}, f32[1,1,2,16384]{3,1,2,0:T(1,128)S(1)}, u32[]{:S(2)}, u32[]{:S(2)}) collective-permute-start(f32[1,1,2,16384]{3,1,2,0:T(1,128)S(1)} %get-tuple-element.119), channel_id=1, source_target_pairs={{0,7},{1,6},{2,5},{3,4},{4,3},{5,2},{6,1},{7,0},{8,15},{9,14},{10,... | collective-permute-start | bytes 393224 | tf_op jit(solution)/shard_map/ppermute | solution.py:25
  299.7 8.7 %collective-permute-start.7 = (f32[1,1,2,16384]{3,1,2,0:T(1,128)S(1)}, f32[1,1,2,16384]{3,1,2,0:T(1,128)S(1)}, u32[]{:S(2)}, u32[]{:S(2)}) collective-permute-start(f32[1,1,2,16384]{3,1,2,0:T(1,128)S(1)} %get-tuple-element.118), channel_id=1, source_target_pairs={{0,8},{1,9},{2,10},{3,11},{4,12},{5,13},{6,14},{7,15},{8,0},{9,1},... | collective-permute-start | bytes 393224 | tf_op jit(solution)/shard_map/ppermute | solution.py:25
  308.3 9.1 %collective-permute-start.8 = (f32[1,1,2,16384]{3,1,2,0:T(1,128)S(1)}, f32[1,1,2,16384]{3,1,2,0:T(1,128)S(1)}, u32[]{:S(2)}, u32[]{:S(2)}) collective-permute-start(f32[1,1,2,16384]{3,1,2,0:T(1,128)S(1)} %get-tuple-element.117), channel_id=1, source_target_pairs={{0,9},{1,8},{2,11},{3,10},{4,13},{5,12},{6,15},{7,14},{8,1},{9,0},... | collective-permute-start | bytes 393224 | tf_op jit(solution)/shard_map/ppermute | solution.py:25
  317.4 8.9 %collective-permute-start.9 = (f32[1,1,2,16384]{3,1,2,0:T(1,128)S(1)}, f32[1,1,2,16384]{3,1,2,0:T(1,128)S(1)}, u32[]{:S(2)}, u32[]{:S(2)}) collective-permute-start(f32[1,1,2,16384]{3,1,2,0:T(1,128)S(1)} %get-tuple-element.116), channel_id=1, source_target_pairs={{0,10},{1,11},{2,8},{3,9},{4,14},{5,15},{6,12},{7,13},{8,2},{9,3},... | collective-permute-start | bytes 393224 | tf_op jit(solution)/shard_map/ppermute | solution.py:25
  326.3 7.7 %collective-permute-start.10 = (f32[1,1,2,16384]{3,1,2,0:T(1,128)S(1)}, f32[1,1,2,16384]{3,1,2,0:T(1,128)S(1)}, u32[]{:S(2)}, u32[]{:S(2)}) collective-permute-start(f32[1,1,2,16384]{3,1,2,0:T(1,128)S(1)} %get-tuple-element.115), channel_id=1, source_target_pairs={{0,11},{1,10},{2,9},{3,8},{4,15},{5,14},{6,13},{7,12},{8,3},{9,2},... | collective-permute-start | bytes 393224 | tf_op jit(solution)/shard_map/ppermute | solution.py:25
  513.9 5.1 copy-start.5
  516.5 3.7 copy-start.6
  516.5 3.7 copy-start.7
  520.2 1.5 copy-start.8
  520.2 2.3 copy-start.9
Sparse Core Ops, SparseCore 0:
  162.8 34.4 all-gather.2
  199.4 33.0 all-gather.4
